TPU v7x, 32 devices: a whole 2x2x4 slice. The times are simulated.
32 devices in a mesh: slab: 8 (over z, y), batch: 4 (over x, core).
Axes of the slice: x: 2, y: 2, z: 4, core: 2. Of those that a mesh axis runs over, the one named last changes fastest.
Arguments:
- velocity_old: float32 [3, 16, 64, 128], P(None, 'slab', 'batch'), may hold values from -40 to 40
- courant: float32 [3, 16, 64, 128], P(None, 'slab', 'batch'), may hold values from -1.5 to 1.5
- cell_ids: int32 [32768], P(('slab', 'batch')), may hold values from 0 to 16383
- forces: float32 [3, 32768], P(None, ('slab', 'batch')), may hold values from -6 to 6
- weights: float32 [32768], P(('slab', 'batch')), may hold values from 0.25 to 4
Outputs:
- velocity_new: float32 [3, 16, 64, 128], P(None, 'slab', 'batch')
- residual: float32 [3, 16, 64, 128], P(None, 'slab', 'batch')
Inputs may be any that keep to these rules, and one draw needn't show every extreme that they name: `cell_ids`: each device's block of 1024 particles lists 1 * 128 particles for each destination slab in turn, slab 0 first.
All inputs are finite; a program needn't handle non-finite values.
Results may differ from a plain program's by a relative error of at most 0.0012.
Values may be sent and summed in bfloat16 or wider, within the bound.
No kernel may reach another device: no remote copies, remote signals or barrier semaphores. Data moves between devices by JAX's collectives and lax.ppermute only.
A program may use at most 64 MiB of HBM per device.

v0:
```python
import math
import jax
import jax.numpy as jnp
from jax import lax
from jax.sharding import PartitionSpec as P

ITERS = 2
diffusion_number = 1.0
diagonal_value = 7.0
deposit_block = 1024


def extended(block, sides, width):
    for axis, dim in sides:
        count = lax.axis_size(axis)
        forward = [(i, i + 1) for i in range(count - 1)]
        backward = [(target, source) for source, target in forward]
        low = lax.ppermute(
            lax.slice_in_dim(block, block.shape[dim] - width, None, axis=dim), axis, forward
        )
        high = lax.ppermute(lax.slice_in_dim(block, 0, width, axis=dim), axis, backward)
        block = jnp.concatenate([low, block, high], axis=dim)
    return block


def inner_product(left, right):
    return jnp.sum(left * right, axis=(1, 2, 3))


def expand(scalars):
    return scalars[:, None, None, None]


def factorize(upper_planes, lower_planes):
    inverses = []
    ratios = []
    for plane_index in range(len(upper_planes)):
        if plane_index == 0:
            pivot_value = diagonal_value + jnp.zeros_like(upper_planes[0])
        else:
            pivot_value = diagonal_value + lower_planes[plane_index] * ratios[-1]
        inverses.append(1.0 / pivot_value)
        ratios.append(-upper_planes[plane_index] * inverses[-1])
    return (inverses, ratios)


def solve_planes(value_planes, inverses, ratios, lower_planes):
    forward = []
    for plane_index in range(len(value_planes)):
        current = value_planes[plane_index]
        if plane_index > 0:
            current = current + lower_planes[plane_index] * forward[-1]
        forward.append(current * inverses[plane_index])
    result = [forward[-1]]
    plane_index = 0
    result.insert(0, forward[plane_index] - ratios[plane_index] * result[0])
    return result


def deposit_rows(cell_ids, momentum, row_total, planes, height, row_width):
    particle_count = cell_ids.shape[0]
    block_size = math.gcd(particle_count, deposit_block)
    row_range = lax.iota(jnp.int32, row_total)
    column_range = lax.iota(jnp.int32, row_width)

    def one_block(iteration, running):
        offset = iteration * block_size
        cell_part = lax.dynamic_slice_in_dim(cell_ids, offset, block_size, 0)
        momentum_part = lax.dynamic_slice_in_dim(momentum, offset, block_size, 1)
        plane_index = cell_part // (height * row_width)
        row_number = cell_part // row_width % height
        column = cell_part % row_width
        local_row = row_number * planes + plane_index
        row_hot = (local_row[:, None] == row_range[None, :]).astype(jnp.bfloat16)
        column_hot = column[:, None] == column_range[None, :]
        spread = jnp.where(
            column_hot[:, None, :], momentum_part.T[:, :, None], jnp.zeros((), jnp.bfloat16)
        )
        spread = spread.reshape(block_size, 3 * row_width)
        return running + jnp.einsum(
            "pr,pc->rc", row_hot, spread, preferred_element_type=jnp.float32
        )

    initial = jnp.zeros((row_total, 3 * row_width), jnp.float32)
    return lax.fori_loop(0, particle_count // block_size, one_block, initial)


def local(velocity_old, courant, cell_ids, forces, weights):
    planes = velocity_old.shape[1]
    rows_quarter = velocity_old.shape[2]
    row_width = velocity_old.shape[3]
    height = rows_quarter * lax.axis_size("batch")
    block_rows = planes * rows_quarter
    momentum = (weights[None, :] * forces).astype(jnp.bfloat16)
    ids_here = lax.all_to_all(cell_ids, "slab", split_axis=0, concat_axis=0, tiled=True)
    moved_momentum = lax.all_to_all(momentum, "slab", split_axis=1, concat_axis=1, tiled=True)
    summed = lax.psum_scatter(
        deposit_rows(
            ids_here, moved_momentum, block_rows * lax.axis_size("batch"), planes, height, row_width
        ),
        "batch",
        scatter_dimension=0,
        tiled=True,
    )
    source = summed.reshape(rows_quarter, planes, 3, row_width).transpose(2, 1, 0, 3)
    right_side = velocity_old + source
    upper = diffusion_number - 0.5 * courant
    lower = diffusion_number + 0.5 * courant
    upper_planes = [upper[0, plane_index] for plane_index in range(planes)]
    lower_planes = [lower[0, plane_index] for plane_index in range(planes)]
    inverses, ratios = factorize(upper_planes, lower_planes)

    def operate(values):
        padded = extended(values, (("slab", 1), ("batch", 2)), 1)
        edge_zeros = jnp.zeros_like(values[..., :1])
        plus_x = jnp.concatenate([values[..., 1:], edge_zeros], axis=3)
        minus_x = jnp.concatenate([edge_zeros, values[..., :-1]], axis=3)
        beside = upper[0] * padded[:, 2:, 1:-1] + lower[0] * padded[:, :-2, 1:-1]
        beside = beside + upper[1] * padded[:, 1:-1, 2:] + lower[1] * padded[:, 1:-1, :-2]
        beside = beside + upper[2] * plus_x + lower[2] * minus_x
        return diagonal_value * values - beside

    def precondition(values):
        value_planes = [values[:, plane_index] for plane_index in range(planes)]
        result = solve_planes(value_planes, inverses, ratios, lower_planes)
        return jnp.stack(result, axis=1)

    solution = jnp.zeros_like(right_side)
    residual = right_side
    direction = right_side
    rho_now = None
    for iteration in range(ITERS):
        precond_dir = precondition(direction)
        image_dir = operate(precond_dir)
        if iteration == 0:
            stacked_terms = jnp.stack(
                [inner_product(right_side, image_dir), inner_product(right_side, residual)], axis=0
            )
        else:
            stacked_terms = inner_product(right_side, image_dir)[None, :]
        gathered_sums = lax.psum(stacked_terms, ("slab", "batch"))
        along_sum = gathered_sums[0]
        if iteration == 0:
            rho_now = gathered_sums[1]
        step_alpha = rho_now / along_sum
        middle = residual - expand(step_alpha) * image_dir
        precond_mid = precondition(middle)
        turned = operate(precond_mid)
        term_list = [inner_product(turned, middle), inner_product(turned, turned)]
        if iteration + 1 < ITERS:
            term_list.append(inner_product(right_side, turned))
        closing_sums = lax.psum(jnp.stack(term_list, axis=0), ("slab", "batch"))
        cross_sum = closing_sums[0]
        square = closing_sums[1]
        shadow_turned = closing_sums[2] if iteration + 1 < ITERS else None
        step_omega = cross_sum / square
        solution = solution + expand(step_alpha) * precond_dir + expand(step_omega) * precond_mid
        residual = middle - expand(step_omega) * turned
        if iteration + 1 < ITERS:
            rho_next = rho_now - step_alpha * along_sum - step_omega * shadow_turned
            factor = rho_next / rho_now * (step_alpha / step_omega)
            direction = residual + expand(factor) * (direction - expand(step_omega) * image_dir)
            rho_now = rho_next
    return (solution, residual)


def solution(mesh):
    placed = (
        P(None, "slab", "batch", None),
        P(None, "slab", "batch", None),
        P(("slab", "batch")),
        P(None, ("slab", "batch")),
        P(("slab", "batch")),
    )
    return jax.shard_map(
        local,
        mesh=mesh,
        in_specs=placed,
        out_specs=(P(None, "slab", "batch", None), P(None, "slab", "batch", None)),
        check_vma=False,
    )
```

profile of v0, /device:TPU:0, one launch (start us, length us, event | category | flops | bytes accessed | tf_op | source)
XLA Modules:
  0.0 286.1 jit_solution(11093976552176510271)
XLA Ops:
  7.2 7.3 %all-to-all-start = ((s32[8,128,1]{1,2,0:T(1,128)}), s32[8,128,1]{1,2,0:T(1,128)S(1)}, u32[]{:S(2)}, u32[]{:S(2)}) async-start(s32[8,128,1]{1,2,0:T(1,128)} %bitcast.93), calls=%async_computation | async-start | bytes 8192 | tf_op jit(solution)/shard_map/all_to_all | solution.py:95
  16.0 5.0 %all-to-all-done = s32[8,128,1]{1,2,0:T(1,128)S(1)} async-done(((s32[8,128,1]{1,2,0:T(1,128)}), s32[8,128,1]{1,2,0:T(1,128)S(1)}, u32[]{:S(2)}, u32[]{:S(2)}) %all-to-all-start) | async-done | bytes 4128 | tf_op jit(solution)/shard_map/all_to_all | solution.py:95
  20.9 3.3 %all-to-all-start.1 = ((bf16[3,8,128]{2,0,1:T(4,128)(2,1)}), bf16[3,8,128]{2,0,1:T(4,128)(2,1)S(1)}, u32[]{:S(2)}, u32[]{:S(2)}) async-start(bf16[3,8,128]{2,0,1:T(4,128)(2,1)} %fusion.48), calls=%async_computation.1 | async-start | bytes 16384 | tf_op jit(solution)/shard_map/all_to_all | solution.py:96
  24.4 6.3 %all-to-all-done.1 = bf16[3,8,128]{2,0,1:T(4,128)(2,1)S(1)} async-done(((bf16[3,8,128]{2,0,1:T(4,128)(2,1)}), bf16[3,8,128]{2,0,1:T(4,128)(2,1)S(1)}, u32[]{:S(2)}, u32[]{:S(2)}) %all-to-all-start.1) | async-done | bytes 6176 | tf_op jit(solution)/shard_map/all_to_all | solution.py:96
  32.1 17.2 %reduce-scatter.2.cloned.1.call-done = f32[32,384]{1,0:T(8,128)} async-done(((f32[128,384]{1,0:T(8,128)}), f32[32,384]{1,0:T(8,128)}) %reduce-scatter.2.cloned.1.call-update) | async-done | bytes 49168 | tf_op jit(solution)/shard_map/reduce_scatter | solution.py:97
  50.2 1.3 collective-permute-start
  51.5 4.5 %collective-permute-start.1 = (f32[3,1,16,128]{3,0,1,2:T(4,128)S(1)}, f32[3,1,16,128]{3,0,1,2:T(4,128)S(1)}, u32[]{:S(2)}, u32[]{:S(2)}) collective-permute-start(f32[3,1,16,128]{3,0,1,2:T(4,128)S(1)} %get-tuple-element.75), channel_id=1, source_target_pairs={{0,4},{4,8},{8,12},{12,16},{16,20},{20,24},{24,28},{1,5},{5,9},{9,... | collective-permute-start | bytes 73736 | tf_op jit(solution)/shard_map/ppermute | solution.py:18
  56.2 1.4 collective-permute-done.1
  57.6 1.3 collective-permute-start.3
  58.9 1.3 collective-permute-start.2
  60.3 2.2 collective-permute-done.2
  62.7 42.7 %psum.28 = f32[2,3]{1,0:T(2,128)S(1)} all-reduce(f32[2,3]{1,0:T(2,128)S(1)} %pad_maximum_fusion.53), channel_id=1, replica_groups=mesh['slab'=8,'batch'=4] {'slab','batch'}, use_global_device_ids=true, to_apply=%region_3.4 | all-reduce | flops 6 | bytes 48 | tf_op jit(solution)/shard_map/psum | solution.py:141
  105.5 1.3 collective-permute-start.4
  106.8 4.8 %collective-permute-start.5 = (f32[3,1,16,128]{3,0,1,2:T(4,128)S(1)}, f32[3,1,16,128]{3,0,1,2:T(4,128)S(1)}, u32[]{:S(2)}, u32[]{:S(2)}) collective-permute-start(f32[3,1,16,128]{3,0,1,2:T(4,128)S(1)} %get-tuple-element.72), channel_id=1, source_target_pairs={{0,4},{4,8},{8,12},{12,16},{16,20},{20,24},{24,28},{1,5},{5,9},{9,... | collective-permute-start | bytes 73736 | tf_op jit(solution)/shard_map/ppermute | solution.py:18
  111.7 1.6 collective-permute-done.5
  113.2 1.3 collective-permute-start.7
  114.5 1.3 collective-permute-start.6
  115.9 3.9 %collective-permute-done.6 = f32[3,4,1,128]{3,0,1,2:T(4,128)S(1)} collective-permute-done((f32[3,4,1,128]{3,0,1,2:T(4,128)S(1)}, f32[3,4,1,128]{3,0,1,2:T(4,128)S(1)}, u32[]{:S(2)}, u32[]{:S(2)}) %collective-permute-start.6) | collective-permute-done | bytes 6176 | tf_op jit(solution)/shard_map/ppermute | solution.py:21
  120.2 42.8 %psum.29 = f32[3,3]{1,0:T(4,128)S(1)} all-reduce(f32[3,3]{1,0:T(4,128)S(1)} %pad_maximum_fusion.52), channel_id=1, replica_groups=mesh['slab'=8,'batch'=4] {'slab','batch'}, use_global_device_ids=true, to_apply=%region_7.8 | all-reduce | flops 9 | bytes 72 | tf_op jit(solution)/shard_map/psum | solution.py:152
  163.1 1.3 collective-permute-start.8
  164.4 4.8 %collective-permute-start.9 = (f32[3,1,16,128]{3,0,1,2:T(4,128)S(1)}, f32[3,1,16,128]{3,0,1,2:T(4,128)S(1)}, u32[]{:S(2)}, u32[]{:S(2)}) collective-permute-start(f32[3,1,16,128]{3,0,1,2:T(4,128)S(1)} %get-tuple-element.66), channel_id=1, source_target_pairs={{0,4},{4,8},{8,12},{12,16},{16,20},{20,24},{24,28},{1,5},{5,9},{9,... | collective-permute-start | bytes 73736 | tf_op jit(solution)/shard_map/ppermute | solution.py:18
  169.3 1.6 collective-permute-done.9
  170.8 1.3 collective-permute-start.11
  172.1 1.3 collective-permute-start.10
  173.5 3.9 %collective-permute-done.10 = f32[3,4,1,128]{3,0,1,2:T(4,128)S(1)} collective-permute-done((f32[3,4,1,128]{3,0,1,2:T(4,128)S(1)}, f32[3,4,1,128]{3,0,1,2:T(4,128)S(1)}, u32[]{:S(2)}, u32[]{:S(2)}) %collective-permute-start.10) | collective-permute-done | bytes 6176 | tf_op jit(solution)/shard_map/ppermute | solution.py:21
  177.7 42.8 %psum.30 = f32[3]{0:T(128)S(1)} all-reduce(f32[3]{0:T(128)S(1)} %get-tuple-element.63), channel_id=1, replica_groups=mesh['slab'=8,'batch'=4] {'slab','batch'}, use_global_device_ids=true, to_apply=%region_9.10 | all-reduce | flops 3 | bytes 24 | tf_op jit(solution)/shard_map/psum | solution.py:141
  220.6 1.3 collective-permute-start.12
  221.9 4.8 %collective-permute-start.13 = (f32[3,1,16,128]{3,0,1,2:T(4,128)S(1)}, f32[3,1,16,128]{3,0,1,2:T(4,128)S(1)}, u32[]{:S(2)}, u32[]{:S(2)}) collective-permute-start(f32[3,1,16,128]{3,0,1,2:T(4,128)S(1)} %get-tuple-element.62), channel_id=1, source_target_pairs={{0,4},{4,8},{8,12},{12,16},{16,20},{20,24},{24,28},{1,5},{5,9},{9,... | collective-permute-start | bytes 73736 | tf_op jit(solution)/shard_map/ppermute | solution.py:18
  226.7 1.6 collective-permute-done.13
  229.6 1.3 collective-permute-start.14
  231.0 3.9 %collective-permute-done.14 = f32[3,4,1,128]{3,0,1,2:T(4,128)S(1)} collective-permute-done((f32[3,4,1,128]{3,0,1,2:T(4,128)S(1)}, f32[3,4,1,128]{3,0,1,2:T(4,128)S(1)}, u32[]{:S(2)}, u32[]{:S(2)}) %collective-permute-start.14) | collective-permute-done | bytes 6176 | tf_op jit(solution)/shard_map/ppermute | solution.py:21
  235.1 42.7 %psum.31 = f32[2,3]{1,0:T(2,128)S(1)} all-reduce(f32[2,3]{1,0:T(2,128)S(1)} %pad_maximum_fusion.54), channel_id=1, replica_groups=mesh['slab'=8,'batch'=4] {'slab','batch'}, use_global_device_ids=true, to_apply=%region_12.13 | all-reduce | flops 6 | bytes 48 | tf_op jit(solution)/shard_map/psum | solution.py:152
  (63 shorter events, 8.4 us)
Async XLA Ops:
  7.2 13.7 %all-to-all-start = ((s32[8,128,1]{1,2,0:T(1,128)}), s32[8,128,1]{1,2,0:T(1,128)S(1)}, u32[]{:S(2)}, u32[]{:S(2)}) async-start(s32[8,128,1]{1,2,0:T(1,128)} %bitcast.93), calls=%async_computation | async-start | bytes 8192 | tf_op jit(solution)/shard_map/all_to_all | solution.py:95
  14.5 0.8 copy-start.1
  14.5 0.8 copy-start.2
  20.9 9.8 %all-to-all-start.1 = ((bf16[3,8,128]{2,0,1:T(4,128)(2,1)}), bf16[3,8,128]{2,0,1:T(4,128)(2,1)S(1)}, u32[]{:S(2)}, u32[]{:S(2)}) async-start(bf16[3,8,128]{2,0,1:T(4,128)(2,1)} %fusion.48), calls=%async_computation.1 | async-start | bytes 16384 | tf_op jit(solution)/shard_map/all_to_all | solution.py:96
  24.2 25.0 %reduce-scatter.2.cloned.1.call-start = ((), (), s32[]{:S(2)}) async-start(), calls=%async_computation.3 | async-start | bytes 245760 | tf_op jit(solution)/shard_map/reduce_scatter | solution.py:97
  32.1 18.0 %copy-start = (f32[3,2,16,128]{3,2,1,0:T(8,128)S(1)}, f32[3,2,16,128]{3,2,1,0:T(8,128)}, u32[]{:S(2)}) copy-start(f32[3,2,16,128]{3,2,1,0:T(8,128)} %param.5) | copy-start | bytes 147460
  50.2 6.0 %collective-permute-start = (f32[3,1,16,128]{3,0,1,2:T(4,128)S(1)}, f32[3,1,16,128]{3,0,1,2:T(4,128)S(1)}, u32[]{:S(2)}, u32[]{:S(2)}) collective-permute-start(f32[3,1,16,128]{3,0,1,2:T(4,128)S(1)} %get-tuple-element.74), channel_id=1, source_target_pairs={{4,0},{8,4},{12,8},{16,12},{20,16},{24,20},{28,24},{5,1},{9,5},{13... | collective-permute-start | bytes 73736 | tf_op jit(solution)/shard_map/ppermute | solution.py:21
  51.5 6.1 %collective-permute-start.1 = (f32[3,1,16,128]{3,0,1,2:T(4,128)S(1)}, f32[3,1,16,128]{3,0,1,2:T(4,128)S(1)}, u32[]{:S(2)}, u32[]{:S(2)}) collective-permute-start(f32[3,1,16,128]{3,0,1,2:T(4,128)S(1)} %get-tuple-element.75), channel_id=1, source_target_pairs={{0,4},{4,8},{8,12},{12,16},{16,20},{20,24},{24,28},{1,5},{5,9},{9,... | collective-permute-start | bytes 73736 | tf_op jit(solution)/shard_map/ppermute | solution.py:18
  57.6 2.7 collective-permute-start.3
  58.9 3.6 %collective-permute-start.2 = (f32[3,4,1,128]{3,0,1,2:T(4,128)S(1)}, f32[3,4,1,128]{3,0,1,2:T(4,128)S(1)}, u32[]{:S(2)}, u32[]{:S(2)}) collective-permute-start(f32[3,4,1,128]{3,0,1,2:T(4,128)S(1)} %get-tuple-element.82), channel_id=1, source_target_pairs={{1,0},{2,1},{3,2},{5,4},{6,5},{7,6},{9,8},{10,9},{11,10},{13,12},{... | collective-permute-start | bytes 18440 | tf_op jit(solution)/shard_map/ppermute | solution.py:21
  105.5 6.1 %collective-permute-start.4 = (f32[3,1,16,128]{3,0,1,2:T(4,128)S(1)}, f32[3,1,16,128]{3,0,1,2:T(4,128)S(1)}, u32[]{:S(2)}, u32[]{:S(2)}) collective-permute-start(f32[3,1,16,128]{3,0,1,2:T(4,128)S(1)} %get-tuple-element.71), channel_id=1, source_target_pairs={{4,0},{8,4},{12,8},{16,12},{20,16},{24,20},{28,24},{5,1},{9,5},{13... | collective-permute-start | bytes 73736 | tf_op jit(solution)/shard_map/ppermute | solution.py:21
  106.8 6.4 %collective-permute-start.5 = (f32[3,1,16,128]{3,0,1,2:T(4,128)S(1)}, f32[3,1,16,128]{3,0,1,2:T(4,128)S(1)}, u32[]{:S(2)}, u32[]{:S(2)}) collective-permute-start(f32[3,1,16,128]{3,0,1,2:T(4,128)S(1)} %get-tuple-element.72), channel_id=1, source_target_pairs={{0,4},{4,8},{8,12},{12,16},{16,20},{20,24},{24,28},{1,5},{5,9},{9,... | collective-permute-start | bytes 73736 | tf_op jit(solution)/shard_map/ppermute | solution.py:18
  113.2 2.7 collective-permute-start.7
  114.5 5.3 %collective-permute-start.6 = (f32[3,4,1,128]{3,0,1,2:T(4,128)S(1)}, f32[3,4,1,128]{3,0,1,2:T(4,128)S(1)}, u32[]{:S(2)}, u32[]{:S(2)}) collective-permute-start(f32[3,4,1,128]{3,0,1,2:T(4,128)S(1)} %get-tuple-element.80), channel_id=1, source_target_pairs={{1,0},{2,1},{3,2},{5,4},{6,5},{7,6},{9,8},{10,9},{11,10},{13,12},{... | collective-permute-start | bytes 18440 | tf_op jit(solution)/shard_map/ppermute | solution.py:21
  163.1 6.1 %collective-permute-start.8 = (f32[3,1,16,128]{3,0,1,2:T(4,128)S(1)}, f32[3,1,16,128]{3,0,1,2:T(4,128)S(1)}, u32[]{:S(2)}, u32[]{:S(2)}) collective-permute-start(f32[3,1,16,128]{3,0,1,2:T(4,128)S(1)} %get-tuple-element.65), channel_id=1, source_target_pairs={{4,0},{8,4},{12,8},{16,12},{20,16},{24,20},{28,24},{5,1},{9,5},{13... | collective-permute-start | bytes 73736 | tf_op jit(solution)/shard_map/ppermute | solution.py:21
  164.4 6.4 %collective-permute-start.9 = (f32[3,1,16,128]{3,0,1,2:T(4,128)S(1)}, f32[3,1,16,128]{3,0,1,2:T(4,128)S(1)}, u32[]{:S(2)}, u32[]{:S(2)}) collective-permute-start(f32[3,1,16,128]{3,0,1,2:T(4,128)S(1)} %get-tuple-element.66), channel_id=1, source_target_pairs={{0,4},{4,8},{8,12},{12,16},{16,20},{20,24},{24,28},{1,5},{5,9},{9,... | collective-permute-start | bytes 73736 | tf_op jit(solution)/shard_map/ppermute | solution.py:18
  170.8 2.7 collective-permute-start.11
  172.1 5.3 %collective-permute-start.10 = (f32[3,4,1,128]{3,0,1,2:T(4,128)S(1)}, f32[3,4,1,128]{3,0,1,2:T(4,128)S(1)}, u32[]{:S(2)}, u32[]{:S(2)}) collective-permute-start(f32[3,4,1,128]{3,0,1,2:T(4,128)S(1)} %get-tuple-element.78), channel_id=1, source_target_pairs={{1,0},{2,1},{3,2},{5,4},{6,5},{7,6},{9,8},{10,9},{11,10},{13,12},{... | collective-permute-start | bytes 18440 | tf_op jit(solution)/shard_map/ppermute | solution.py:21
  220.6 6.1 %collective-permute-start.12 = (f32[3,1,16,128]{3,0,1,2:T(4,128)S(1)}, f32[3,1,16,128]{3,0,1,2:T(4,128)S(1)}, u32[]{:S(2)}, u32[]{:S(2)}) collective-permute-start(f32[3,1,16,128]{3,0,1,2:T(4,128)S(1)} %get-tuple-element.61), channel_id=1, source_target_pairs={{4,0},{8,4},{12,8},{16,12},{20,16},{24,20},{28,24},{5,1},{9,5},{13... | collective-permute-start | bytes 73736 | tf_op jit(solution)/shard_map/ppermute | solution.py:21
  221.9 6.4 %collective-permute-start.13 = (f32[3,1,16,128]{3,0,1,2:T(4,128)S(1)}, f32[3,1,16,128]{3,0,1,2:T(4,128)S(1)}, u32[]{:S(2)}, u32[]{:S(2)}) collective-permute-start(f32[3,1,16,128]{3,0,1,2:T(4,128)S(1)} %get-tuple-element.62), channel_id=1, source_target_pairs={{0,4},{4,8},{8,12},{12,16},{16,20},{20,24},{24,28},{1,5},{5,9},{9,... | collective-permute-start | bytes 73736 | tf_op jit(solution)/shard_map/ppermute | solution.py:18
  228.3 2.7 collective-permute-start.15
  229.6 5.3 %collective-permute-start.14 = (f32[3,4,1,128]{3,0,1,2:T(4,128)S(1)}, f32[3,4,1,128]{3,0,1,2:T(4,128)S(1)}, u32[]{:S(2)}, u32[]{:S(2)}) collective-permute-start(f32[3,4,1,128]{3,0,1,2:T(4,128)S(1)} %get-tuple-element.76), channel_id=1, source_target_pairs={{1,0},{2,1},{3,2},{5,4},{6,5},{7,6},{9,8},{10,9},{11,10},{13,12},{... | collective-permute-start | bytes 18440 | tf_op jit(solution)/shard_map/ppermute | solution.py:21
Sparse Core Ops, SparseCore 0:
  32.2 17.0 reduce-scatter.1
where the time goes:
time: 287 us; the launch traced here: 286 us
  blocking collectives  171 us (60%)
  waiting for transfers between devices  48.5 us (17%)
  starting transfers between devices  45.1 us (16%)
  between operations  14.5 us (5%)
  other arithmetic  3.66 us (1%)
    psum x2, blocking collectives, local(): closing_sums = lax.psum(jnp.stack(term_list, axis=0), ('slab', 'batch'))  85.6 us
    psum x2, blocking collectives, local(): gathered_sums = lax.psum(stacked_terms, ('slab', 'batch'))  85.4 us
    ppermute x8, starting transfers between devices, extended(): lax.ppermute(lax.slice_in_dim(block, block.shape[dim] - width, None, axis...  24.1 us
    reduce_scatter x1, waiting for transfers between devices, local(): lax.psum_scatter(deposit_rows(ids_here, moved_momentum, block_rows * lax....  17.2 us
    ppermute x8, waiting for transfers between devices, extended(): lax.ppermute(lax.slice_in_dim(block, 0, width, axis=dim), axis, backward)  13.9 us
    ppermute x8, starting transfers between devices, extended(): lax.ppermute(lax.slice_in_dim(block, 0, width, axis=dim), axis, backward)  10.3 us
    all_to_all x1, starting transfers between devices, local(): lax.all_to_all(cell_ids, 'slab', split_axis=0, concat_axis=0, tiled=True)  7.32 us
    all_to_all x1, waiting for transfers between devices, local(): lax.all_to_all(momentum, 'slab', split_axis=1, concat_axis=1, tiled=True)  6.3 us
  transfers between devices with their start and end apart: 19, of which 11 were waited for; matrix products, arithmetic and copies ran while one was open for 1% of the time, Pallas kernels for 0%

commit v1 on v0

--- a/solution.py
+++ b/solution.py
@@ -3,6 +3,7 @@
 import jax.numpy as jnp
 from jax import lax
 from jax.sharding import PartitionSpec as P
+from jax.lax import psum
 
 ITERS = 2
 diffusion_number = 1.0
@@ -149,7 +150,9 @@
         term_list = [inner_product(turned, middle), inner_product(turned, turned)]
         if iteration + 1 < ITERS:
             term_list.append(inner_product(right_side, turned))
-        closing_sums = lax.psum(jnp.stack(term_list, axis=0), ("slab", "batch"))
+        mat = jnp.stack(term_list, axis=0)
+        all_rows = psum(mat, axis_name="batch")
+        closing_sums = psum(all_rows, axis_name="slab")
         cross_sum = closing_sums[0]
         square = closing_sums[1]
         shadow_turned = closing_sums[2] if iteration + 1 < ITERS else None

time: 287 us -> 258 us (0.90)
  blocking collectives: 171 us -> 142 us
    psum x2 -> x4, blocking collectives: 85.6 us -> 58.7 us  [the longest x2 42.6 us: local(): closing_sums = psum(all_rows, axis_name='slab')]
where the time goes in v1:
time: 258 us; the launch traced here: 257 us
  blocking collectives  142 us (55%)
  waiting for transfers between devices  48.1 us (19%)
  starting transfers between devices  44.8 us (17%)
  between operations  14.5 us (6%)
  other arithmetic  3.66 us (1%)
    psum x2, blocking collectives, local(): gathered_sums = lax.psum(stacked_terms, ('slab', 'batch'))  83.5 us
    psum x2, blocking collectives, local(): closing_sums = psum(all_rows, axis_name='slab')  42.6 us
    ppermute x8, starting transfers between devices, extended(): lax.ppermute(lax.slice_in_dim(block, block.shape[dim] - width, None, axis...  23.8 us
    reduce_scatter x1, waiting for transfers between devices, local(): lax.psum_scatter(deposit_rows(ids_here, moved_momentum, block_rows * lax....  17.2 us
    psum x2, blocking collectives, local(): all_rows = psum(mat, axis_name='batch')  16.1 us
    ppermute x8, waiting for transfers between devices, extended(): lax.ppermute(lax.slice_in_dim(block, 0, width, axis=dim), axis, backward)  13.5 us
    ppermute x8, starting transfers between devices, extended(): lax.ppermute(lax.slice_in_dim(block, 0, width, axis=dim), axis, backward)  10.3 us
    all_to_all x1, starting transfers between devices, local(): lax.all_to_all(cell_ids, 'slab', split_axis=0, concat_axis=0, tiled=True)  7.32 us
  transfers between devices with their start and end apart: 19, of which 11 were waited for; matrix products, arithmetic and copies ran while one was open for 1% of the time, Pallas kernels for 0%

profile of v1, /device:TPU:0, one launch (start us, length us, event | category | flops | bytes accessed | tf_op | source)
XLA Modules:
  0.0 256.7 jit_solution(35111873674021365)
XLA Ops:
  7.2 7.3 %all-to-all-start = ((s32[8,128,1]{1,2,0:T(1,128)}), s32[8,128,1]{1,2,0:T(1,128)S(1)}, u32[]{:S(2)}, u32[]{:S(2)}) async-start(s32[8,128,1]{1,2,0:T(1,128)} %bitcast.93), calls=%async_computation | async-start | bytes 8192 | tf_op jit(solution)/shard_map/all_to_all | solution.py:96
  16.0 5.0 %all-to-all-done = s32[8,128,1]{1,2,0:T(1,128)S(1)} async-done(((s32[8,128,1]{1,2,0:T(1,128)}), s32[8,128,1]{1,2,0:T(1,128)S(1)}, u32[]{:S(2)}, u32[]{:S(2)}) %all-to-all-start) | async-done | bytes 4128 | tf_op jit(solution)/shard_map/all_to_all | solution.py:96
  20.9 3.3 %all-to-all-start.1 = ((bf16[3,8,128]{2,0,1:T(4,128)(2,1)}), bf16[3,8,128]{2,0,1:T(4,128)(2,1)S(1)}, u32[]{:S(2)}, u32[]{:S(2)}) async-start(bf16[3,8,128]{2,0,1:T(4,128)(2,1)} %fusion.48), calls=%async_computation.1 | async-start | bytes 16384 | tf_op jit(solution)/shard_map/all_to_all | solution.py:97
  24.4 6.3 %all-to-all-done.1 = bf16[3,8,128]{2,0,1:T(4,128)(2,1)S(1)} async-done(((bf16[3,8,128]{2,0,1:T(4,128)(2,1)}), bf16[3,8,128]{2,0,1:T(4,128)(2,1)S(1)}, u32[]{:S(2)}, u32[]{:S(2)}) %all-to-all-start.1) | async-done | bytes 6176 | tf_op jit(solution)/shard_map/all_to_all | solution.py:97
  32.1 17.2 %reduce-scatter.2.cloned.1.call-done = f32[32,384]{1,0:T(8,128)} async-done(((f32[128,384]{1,0:T(8,128)}), f32[32,384]{1,0:T(8,128)}) %reduce-scatter.2.cloned.1.call-update) | async-done | bytes 49168 | tf_op jit(solution)/shard_map/reduce_scatter | solution.py:98
  50.2 1.3 collective-permute-start
  51.5 4.5 %collective-permute-start.1 = (f32[3,1,16,128]{3,0,1,2:T(4,128)S(1)}, f32[3,1,16,128]{3,0,1,2:T(4,128)S(1)}, u32[]{:S(2)}, u32[]{:S(2)}) collective-permute-start(f32[3,1,16,128]{3,0,1,2:T(4,128)S(1)} %get-tuple-element.75), channel_id=1, source_target_pairs={{0,4},{4,8},{8,12},{12,16},{16,20},{20,24},{24,28},{1,5},{5,9},{9,... | collective-permute-start | bytes 73736 | tf_op jit(solution)/shard_map/ppermute | solution.py:19
  56.2 1.4 collective-permute-done.1
  57.6 1.3 collective-permute-start.3
  58.9 1.3 collective-permute-start.2
  60.3 2.2 collective-permute-done.2
  62.7 42.6 %psum.42 = f32[2,3]{1,0:T(2,128)S(1)} all-reduce(f32[2,3]{1,0:T(2,128)S(1)} %pad_maximum_fusion.53), channel_id=1, replica_groups=mesh['slab'=8,'batch'=4] {'slab','batch'}, use_global_device_ids=true, to_apply=%region_3.4 | all-reduce | flops 6 | bytes 48 | tf_op jit(solution)/shard_map/psum | solution.py:142
  105.5 1.3 collective-permute-start.4
  106.8 4.8 %collective-permute-start.5 = (f32[3,1,16,128]{3,0,1,2:T(4,128)S(1)}, f32[3,1,16,128]{3,0,1,2:T(4,128)S(1)}, u32[]{:S(2)}, u32[]{:S(2)}) collective-permute-start(f32[3,1,16,128]{3,0,1,2:T(4,128)S(1)} %get-tuple-element.72), channel_id=1, source_target_pairs={{0,4},{4,8},{8,12},{12,16},{16,20},{20,24},{24,28},{1,5},{5,9},{9,... | collective-permute-start | bytes 73736 | tf_op jit(solution)/shard_map/ppermute | solution.py:19
  111.6 1.6 collective-permute-done.5
  114.5 1.3 collective-permute-start.6
  115.9 3.9 %collective-permute-done.6 = f32[3,4,1,128]{3,0,1,2:T(4,128)S(1)} collective-permute-done((f32[3,4,1,128]{3,0,1,2:T(4,128)S(1)}, f32[3,4,1,128]{3,0,1,2:T(4,128)S(1)}, u32[]{:S(2)}, u32[]{:S(2)}) %collective-permute-start.6) | collective-permute-done | bytes 6176 | tf_op jit(solution)/shard_map/ppermute | solution.py:22
  120.1 8.1 %psum.43 = f32[3,3]{1,0:T(4,128)S(1)} all-reduce(f32[3,3]{1,0:T(4,128)S(1)} %pad_maximum_fusion.52), channel_id=1, replica_groups=mesh['slab'=8,'batch'=4] {'batch'}, use_global_device_ids=true, to_apply=%region_7.8 | all-reduce | flops 9 | bytes 72 | tf_op jit(solution)/shard_map/psum | solution.py:154
  128.2 22.2 %psum.44 = f32[3,3]{1,0:T(4,128)S(1)} all-reduce(f32[3,3]{1,0:T(4,128)S(1)} %psum.43), channel_id=1, replica_groups=mesh['slab'=8,'batch'=4] {'slab'}, use_global_device_ids=true, to_apply=%region_8.9 | all-reduce | flops 9 | bytes 72 | tf_op jit(solution)/shard_map/psum | solution.py:155
  150.5 1.3 collective-permute-start.8
  151.8 4.5 %collective-permute-start.9 = (f32[3,1,16,128]{3,0,1,2:T(4,128)S(1)}, f32[3,1,16,128]{3,0,1,2:T(4,128)S(1)}, u32[]{:S(2)}, u32[]{:S(2)}) collective-permute-start(f32[3,1,16,128]{3,0,1,2:T(4,128)S(1)} %get-tuple-element.66), channel_id=1, source_target_pairs={{0,4},{4,8},{8,12},{12,16},{16,20},{20,24},{24,28},{1,5},{5,9},{9,... | collective-permute-start | bytes 73736 | tf_op jit(solution)/shard_map/ppermute | solution.py:19
  156.3 1.6 collective-permute-done.9
  159.2 1.3 collective-permute-start.10
  160.6 3.5 %collective-permute-done.10 = f32[3,4,1,128]{3,0,1,2:T(4,128)S(1)} collective-permute-done((f32[3,4,1,128]{3,0,1,2:T(4,128)S(1)}, f32[3,4,1,128]{3,0,1,2:T(4,128)S(1)}, u32[]{:S(2)}, u32[]{:S(2)}) %collective-permute-start.10) | collective-permute-done | bytes 6176 | tf_op jit(solution)/shard_map/ppermute | solution.py:22
  164.4 40.9 %psum.45 = f32[3]{0:T(128)S(1)} all-reduce(f32[3]{0:T(128)S(1)} %get-tuple-element.63), channel_id=1, replica_groups=mesh['slab'=8,'batch'=4] {'slab','batch'}, use_global_device_ids=true, to_apply=%region_10.11 | all-reduce | flops 3 | bytes 24 | tf_op jit(solution)/shard_map/psum | solution.py:142
  205.5 1.3 collective-permute-start.12
  206.8 4.8 %collective-permute-start.13 = (f32[3,1,16,128]{3,0,1,2:T(4,128)S(1)}, f32[3,1,16,128]{3,0,1,2:T(4,128)S(1)}, u32[]{:S(2)}, u32[]{:S(2)}) collective-permute-start(f32[3,1,16,128]{3,0,1,2:T(4,128)S(1)} %get-tuple-element.62), channel_id=1, source_target_pairs={{0,4},{4,8},{8,12},{12,16},{16,20},{20,24},{24,28},{1,5},{5,9},{9,... | collective-permute-start | bytes 73736 | tf_op jit(solution)/shard_map/ppermute | solution.py:19
  211.6 1.6 collective-permute-done.13
  214.4 1.3 collective-permute-start.14
  215.8 3.9 %collective-permute-done.14 = f32[3,4,1,128]{3,0,1,2:T(4,128)S(1)} collective-permute-done((f32[3,4,1,128]{3,0,1,2:T(4,128)S(1)}, f32[3,4,1,128]{3,0,1,2:T(4,128)S(1)}, u32[]{:S(2)}, u32[]{:S(2)}) %collective-permute-start.14) | collective-permute-done | bytes 6176 | tf_op jit(solution)/shard_map/ppermute | solution.py:22
  220.0 8.1 %psum.46 = f32[2,3]{1,0:T(2,128)S(1)} all-reduce(f32[2,3]{1,0:T(2,128)S(1)} %pad_maximum_fusion.54), channel_id=1, replica_groups=mesh['slab'=8,'batch'=4] {'batch'}, use_global_device_ids=true, to_apply=%region_13.14 | all-reduce | flops 6 | bytes 48 | tf_op jit(solution)/shard_map/psum | solution.py:154
  228.1 20.4 %psum.47 = f32[2,3]{1,0:T(2,128)S(1)} all-reduce(f32[2,3]{1,0:T(2,128)S(1)} %psum.46), channel_id=1, replica_groups=mesh['slab'=8,'batch'=4] {'slab'}, use_global_device_ids=true, to_apply=%region_14.15 | all-reduce | flops 6 | bytes 48 | tf_op jit(solution)/shard_map/psum | solution.py:155
  (65 shorter events, 11.0 us)
Async XLA Ops:
  7.2 13.7 %all-to-all-start = ((s32[8,128,1]{1,2,0:T(1,128)}), s32[8,128,1]{1,2,0:T(1,128)S(1)}, u32[]{:S(2)}, u32[]{:S(2)}) async-start(s32[8,128,1]{1,2,0:T(1,128)} %bitcast.93), calls=%async_computation | async-start | bytes 8192 | tf_op jit(solution)/shard_map/all_to_all | solution.py:96
  14.5 0.8 copy-start.1
  14.5 0.8 copy-start.2
  20.9 9.8 %all-to-all-start.1 = ((bf16[3,8,128]{2,0,1:T(4,128)(2,1)}), bf16[3,8,128]{2,0,1:T(4,128)(2,1)S(1)}, u32[]{:S(2)}, u32[]{:S(2)}) async-start(bf16[3,8,128]{2,0,1:T(4,128)(2,1)} %fusion.48), calls=%async_computation.1 | async-start | bytes 16384 | tf_op jit(solution)/shard_map/all_to_all | solution.py:97
  24.2 25.0 %reduce-scatter.2.cloned.1.call-start = ((), (), s32[]{:S(2)}) async-start(), calls=%async_computation.3 | async-start | bytes 245760 | tf_op jit(solution)/shard_map/reduce_scatter | solution.py:98
  32.1 18.0 %copy-start = (f32[3,2,16,128]{3,2,1,0:T(8,128)S(1)}, f32[3,2,16,128]{3,2,1,0:T(8,128)}, u32[]{:S(2)}) copy-start(f32[3,2,16,128]{3,2,1,0:T(8,128)} %param.5) | copy-start | bytes 147460
  50.2 6.0 %collective-permute-start = (f32[3,1,16,128]{3,0,1,2:T(4,128)S(1)}, f32[3,1,16,128]{3,0,1,2:T(4,128)S(1)}, u32[]{:S(2)}, u32[]{:S(2)}) collective-permute-start(f32[3,1,16,128]{3,0,1,2:T(4,128)S(1)} %get-tuple-element.74), channel_id=1, source_target_pairs={{4,0},{8,4},{12,8},{16,12},{20,16},{24,20},{28,24},{5,1},{9,5},{13... | collective-permute-start | bytes 73736 | tf_op jit(solution)/shard_map/ppermute | solution.py:22
  51.5 6.1 %collective-permute-start.1 = (f32[3,1,16,128]{3,0,1,2:T(4,128)S(1)}, f32[3,1,16,128]{3,0,1,2:T(4,128)S(1)}, u32[]{:S(2)}, u32[]{:S(2)}) collective-permute-start(f32[3,1,16,128]{3,0,1,2:T(4,128)S(1)} %get-tuple-element.75), channel_id=1, source_target_pairs={{0,4},{4,8},{8,12},{12,16},{16,20},{20,24},{24,28},{1,5},{5,9},{9,... | collective-permute-start | bytes 73736 | tf_op jit(solution)/shard_map/ppermute | solution.py:19
  57.6 2.7 %collective-permute-start.3 = (f32[3,4,1,128]{3,0,1,2:T(4,128)S(1)}, f32[3,4,1,128]{3,0,1,2:T(4,128)S(1)}, u32[]{:S(2)}, u32[]{:S(2)}) collective-permute-start(f32[3,4,1,128]{3,0,1,2:T(4,128)S(1)} %get-tuple-element.83), channel_id=1, source_target_pairs={{0,1},{1,2},{2,3},{4,5},{5,6},{6,7},{8,9},{9,10},{10,11},{12,13},{... | collective-permute-start | bytes 18440 | tf_op jit(solution)/shard_map/ppermute | solution.py:19
  58.9 3.6 %collective-permute-start.2 = (f32[3,4,1,128]{3,0,1,2:T(4,128)S(1)}, f32[3,4,1,128]{3,0,1,2:T(4,128)S(1)}, u32[]{:S(2)}, u32[]{:S(2)}) collective-permute-start(f32[3,4,1,128]{3,0,1,2:T(4,128)S(1)} %get-tuple-element.82), channel_id=1, source_target_pairs={{1,0},{2,1},{3,2},{5,4},{6,5},{7,6},{9,8},{10,9},{11,10},{13,12},{... | collective-permute-start | bytes 18440 | tf_op jit(solution)/shard_map/ppermute | solution.py:22
  105.5 6.1 %collective-permute-start.4 = (f32[3,1,16,128]{3,0,1,2:T(4,128)S(1)}, f32[3,1,16,128]{3,0,1,2:T(4,128)S(1)}, u32[]{:S(2)}, u32[]{:S(2)}) collective-permute-start(f32[3,1,16,128]{3,0,1,2:T(4,128)S(1)} %get-tuple-element.71), channel_id=1, source_target_pairs={{4,0},{8,4},{12,8},{16,12},{20,16},{24,20},{28,24},{5,1},{9,5},{13... | collective-permute-start | bytes 73736 | tf_op jit(solution)/shard_map/ppermute | solution.py:22
  106.8 6.4 %collective-permute-start.5 = (f32[3,1,16,128]{3,0,1,2:T(4,128)S(1)}, f32[3,1,16,128]{3,0,1,2:T(4,128)S(1)}, u32[]{:S(2)}, u32[]{:S(2)}) collective-permute-start(f32[3,1,16,128]{3,0,1,2:T(4,128)S(1)} %get-tuple-element.72), channel_id=1, source_target_pairs={{0,4},{4,8},{8,12},{12,16},{16,20},{20,24},{24,28},{1,5},{5,9},{9,... | collective-permute-start | bytes 73736 | tf_op jit(solution)/shard_map/ppermute | solution.py:19
  113.2 2.7 %collective-permute-start.7 = (f32[3,4,1,128]{3,0,1,2:T(4,128)S(1)}, f32[3,4,1,128]{3,0,1,2:T(4,128)S(1)}, u32[]{:S(2)}, u32[]{:S(2)}) collective-permute-start(f32[3,4,1,128]{3,0,1,2:T(4,128)S(1)} %get-tuple-element.81), channel_id=1, source_target_pairs={{0,1},{1,2},{2,3},{4,5},{5,6},{6,7},{8,9},{9,10},{10,11},{12,13},{... | collective-permute-start | bytes 18440 | tf_op jit(solution)/shard_map/ppermute | solution.py:19
  114.5 5.3 %collective-permute-start.6 = (f32[3,4,1,128]{3,0,1,2:T(4,128)S(1)}, f32[3,4,1,128]{3,0,1,2:T(4,128)S(1)}, u32[]{:S(2)}, u32[]{:S(2)}) collective-permute-start(f32[3,4,1,128]{3,0,1,2:T(4,128)S(1)} %get-tuple-element.80), channel_id=1, source_target_pairs={{1,0},{2,1},{3,2},{5,4},{6,5},{7,6},{9,8},{10,9},{11,10},{13,12},{... | collective-permute-start | bytes 18440 | tf_op jit(solution)/shard_map/ppermute | solution.py:22
  150.5 5.9 %collective-permute-start.8 = (f32[3,1,16,128]{3,0,1,2:T(4,128)S(1)}, f32[3,1,16,128]{3,0,1,2:T(4,128)S(1)}, u32[]{:S(2)}, u32[]{:S(2)}) collective-permute-start(f32[3,1,16,128]{3,0,1,2:T(4,128)S(1)} %get-tuple-element.65), channel_id=1, source_target_pairs={{4,0},{8,4},{12,8},{16,12},{20,16},{24,20},{28,24},{5,1},{9,5},{13... | collective-permute-start | bytes 73736 | tf_op jit(solution)/shard_map/ppermute | solution.py:22
  151.8 6.1 %collective-permute-start.9 = (f32[3,1,16,128]{3,0,1,2:T(4,128)S(1)}, f32[3,1,16,128]{3,0,1,2:T(4,128)S(1)}, u32[]{:S(2)}, u32[]{:S(2)}) collective-permute-start(f32[3,1,16,128]{3,0,1,2:T(4,128)S(1)} %get-tuple-element.66), channel_id=1, source_target_pairs={{0,4},{4,8},{8,12},{12,16},{16,20},{20,24},{24,28},{1,5},{5,9},{9,... | collective-permute-start | bytes 73736 | tf_op jit(solution)/shard_map/ppermute | solution.py:19
  157.9 2.7 %collective-permute-start.11 = (f32[3,4,1,128]{3,0,1,2:T(4,128)S(1)}, f32[3,4,1,128]{3,0,1,2:T(4,128)S(1)}, u32[]{:S(2)}, u32[]{:S(2)}) collective-permute-start(f32[3,4,1,128]{3,0,1,2:T(4,128)S(1)} %get-tuple-element.79), channel_id=1, source_target_pairs={{0,1},{1,2},{2,3},{4,5},{5,6},{6,7},{8,9},{9,10},{10,11},{12,13},{... | collective-permute-start | bytes 18440 | tf_op jit(solution)/shard_map/ppermute | solution.py:19
  159.2 5.0 %collective-permute-start.10 = (f32[3,4,1,128]{3,0,1,2:T(4,128)S(1)}, f32[3,4,1,128]{3,0,1,2:T(4,128)S(1)}, u32[]{:S(2)}, u32[]{:S(2)}) collective-permute-start(f32[3,4,1,128]{3,0,1,2:T(4,128)S(1)} %get-tuple-element.78), channel_id=1, source_target_pairs={{1,0},{2,1},{3,2},{5,4},{6,5},{7,6},{9,8},{10,9},{11,10},{13,12},{... | collective-permute-start | bytes 18440 | tf_op jit(solution)/shard_map/ppermute | solution.py:22
  205.5 6.1 %collective-permute-start.12 = (f32[3,1,16,128]{3,0,1,2:T(4,128)S(1)}, f32[3,1,16,128]{3,0,1,2:T(4,128)S(1)}, u32[]{:S(2)}, u32[]{:S(2)}) collective-permute-start(f32[3,1,16,128]{3,0,1,2:T(4,128)S(1)} %get-tuple-element.61), channel_id=1, source_target_pairs={{4,0},{8,4},{12,8},{16,12},{20,16},{24,20},{28,24},{5,1},{9,5},{13... | collective-permute-start | bytes 73736 | tf_op jit(solution)/shard_map/ppermute | solution.py:22
  206.8 6.4 %collective-permute-start.13 = (f32[3,1,16,128]{3,0,1,2:T(4,128)S(1)}, f32[3,1,16,128]{3,0,1,2:T(4,128)S(1)}, u32[]{:S(2)}, u32[]{:S(2)}) collective-permute-start(f32[3,1,16,128]{3,0,1,2:T(4,128)S(1)} %get-tuple-element.62), channel_id=1, source_target_pairs={{0,4},{4,8},{8,12},{12,16},{16,20},{20,24},{24,28},{1,5},{5,9},{9,... | collective-permute-start | bytes 73736 | tf_op jit(solution)/shard_map/ppermute | solution.py:19
  213.2 2.7 %collective-permute-start.15 = (f32[3,4,1,128]{3,0,1,2:T(4,128)S(1)}, f32[3,4,1,128]{3,0,1,2:T(4,128)S(1)}, u32[]{:S(2)}, u32[]{:S(2)}) collective-permute-start(f32[3,4,1,128]{3,0,1,2:T(4,128)S(1)} %get-tuple-element.77), channel_id=1, source_target_pairs={{0,1},{1,2},{2,3},{4,5},{5,6},{6,7},{8,9},{9,10},{10,11},{12,13},{... | collective-permute-start | bytes 18440 | tf_op jit(solution)/shard_map/ppermute | solution.py:19
  214.4 5.3 %collective-permute-start.14 = (f32[3,4,1,128]{3,0,1,2:T(4,128)S(1)}, f32[3,4,1,128]{3,0,1,2:T(4,128)S(1)}, u32[]{:S(2)}, u32[]{:S(2)}) collective-permute-start(f32[3,4,1,128]{3,0,1,2:T(4,128)S(1)} %get-tuple-element.76), channel_id=1, source_target_pairs={{1,0},{2,1},{3,2},{5,4},{6,5},{7,6},{9,8},{10,9},{11,10},{13,12},{... | collective-permute-start | bytes 18440 | tf_op jit(solution)/shard_map/ppermute | solution.py:22
Sparse Core Ops, SparseCore 0:
  32.2 17.0 reduce-scatter.1
